TPU v7x, 512 devices: a whole 4x4x16 slice. The times are simulated.
512 devices in a mesh: delay: 32 (over y, z_lo), row: 4 (over x), col: 4 (over z_hi, core).
Axes of the slice: x: 4, y: 4, z: 16 (z_hi: 2, z_lo: 8; z = z_hi * 8 + z_lo), core: 2. Of those that a mesh axis runs over, the one named last changes fastest.
Arguments:
- excitation: bfloat16 [2, 3072, 128], P(None, 'row'), may hold values from -6 to 6
- delay_ops: bfloat16 [32, 3072, 3072], P('delay', 'row', 'col'), may hold values from -0.01953125 to 0.01953125
- inverse_op: bfloat16 [3072, 3072], P('col', 'row'), may hold values from -0.109375 to 0.109375
- history: bfloat16 [32, 3072, 128], P('delay', 'col'), may hold values from -6 to 6
Outputs:
- currents: bfloat16 [2, 3072, 128], P(None, 'col')
- final_history: bfloat16 [32, 3072, 128], P('delay', 'col')
All inputs are finite; a program needn't handle non-finite values.
Results may differ from a plain program's by a relative error of at most 0.008.
Values may be sent and summed in bfloat16 or wider, within the bound.
A program may use at most 64 MiB of HBM per device.

v0:
```python
import jax
import jax.numpy as jnp
from jax import lax
from jax.sharding import Mesh
from jax.sharding import PartitionSpec as P

STEPS = 2
DELAY = ("delay_0", "delay_1")
COL = ("col_0", "col_1")


def split_up(shard, dim, count):
    lengths = shard.shape
    pieces = shard.reshape(*lengths[:dim], count, lengths[dim] // count, *lengths[dim + 1 :])
    return jnp.moveaxis(pieces, dim, 0)


def sent_and_summed(shard, axis, dim):
    count = lax.axis_size(axis)
    pieces = lax.all_to_all(split_up(shard, dim, count), axis, 0, 0, tiled=True)
    return jnp.sum(pieces, axis=0)


def laid_out(pieces, dim):
    lengths = list(pieces.shape[1:])
    lengths[dim] *= pieces.shape[0]
    return jnp.moveaxis(pieces, 0, dim).reshape(lengths)


def copy_for_each(shard, axis):
    copies = jnp.broadcast_to(shard, (lax.axis_size(axis), *shard.shape))
    return lax.all_to_all(copies, axis, split_axis=0, concat_axis=0, tiled=True)


def collect(shard, axis, dim):
    return laid_out(copy_for_each(shard, axis), dim)


def sum_in_two_steps(shard, axes, dim):
    far, near = axes
    own = sent_and_summed(split_up(shard, dim, lax.axis_size(far)), near, dim + 1)
    return jnp.sum(lax.all_to_all(own, far, 0, 0, tiled=True), axis=0)


def filled_up(lines, count):
    spare = -len(lines) % count
    return jnp.pad(lines, [(0, spare)] + [(0, 0)] * (lines.ndim - 1))


def whole_of(shard, axes, dim):
    far, near = axes
    first = copy_for_each(shard, far)
    pieces = jnp.swapaxes(copy_for_each(first, near), 0, 1)
    return laid_out(pieces.reshape(-1, *shard.shape), dim)


def sum_by_parts(shard, axes):
    lines = shard.reshape(-1, shard.shape[-1])
    own = sum_in_two_steps(
        filled_up(lines, lax.axis_size(axes[0]) * lax.axis_size(axes[1])), axes, 0
    )
    whole = whole_of(own, axes, 0)
    return whole[: len(lines)].reshape(shard.shape)


def from_behind(block, axis, distance):
    devices = range(lax.axis_size(axis))
    route = [(i - distance, i) for i in devices if i - distance in devices]
    return lax.ppermute(block, axis, route)


def on_device(excitation, delay_ops, inverse_op, history):
    operator = delay_ops[0]
    stored = history[0]
    position = lax.axis_index(DELAY)
    produced = []
    hist = stored
    for step in range(STEPS):
        partial_value = jnp.dot(operator, hist, preferred_element_type=jnp.float32)
        retarded = sum_by_parts(partial_value, (("delay_0", "delay_1", "col_0"), "col_1"))
        rhs = (excitation[step].astype(jnp.float32) - retarded).astype(jnp.bfloat16)
        mine = sent_and_summed(
            jnp.dot(inverse_op, rhs, preferred_element_type=jnp.float32), "row", 0
        ).astype(jnp.bfloat16)
        current = collect(mine, "row", 0)
        shifted = from_behind(hist, DELAY, 1)
        hist = jnp.where(position == 0, current, shifted)
        produced.append(current)
    stacked = jnp.stack(produced)
    return (stacked, hist[None])


def solution(mesh):
    split = Mesh(
        mesh.devices.reshape(4, 8, mesh.shape["row"], 2, 2),
        ("delay_0", "delay_1", "row", "col_0", "col_1"),
    )
    in_specs = (P(None, "row", None), P(DELAY, "row", COL), P(COL, "row"), P(DELAY, COL, None))
    out_specs = (P(None, COL, None), P(DELAY, COL, None))
    return jax.shard_map(
        on_device, mesh=split, in_specs=in_specs, out_specs=out_specs, check_vma=False
    )
```

profile of v0, /device:TPU:10, one launch (start us, length us, event | category | flops | bytes accessed | tf_op | source)
XLA Modules:
  0.0 205.3 jit_solution(4673248921050400444)
XLA Ops:
  0.6 0.0 copy-start
  0.6 2.3 %dot_general.20 = bf16[64,2,6,768]{3,2,1,0:T(8,128)(2,1)S(1)} reshape(bf16[1,768,768]{2,1,0:T(8,128)(2,1)} %param.5) | data formatting | bytes 2359296 | tf_op jit(solution)/shard_map/dot_general | solution.py:79
  3.0 1.5 convolution_bitcast_fusion.3
  4.5 4.0 %all_to_all.60 = f32[2,64,6,128]{3,1,2,0:T(8,128)S(1)} all-to-all(f32[2,64,6,128]{3,1,2,0:T(8,128)S(1)} %convolution_bitcast_fusion.3), channel_id=1, replica_groups=mesh['delay_0'=4,'delay_1'=8,'row'=4,'col_0'=2,'col_1'=2] {'col_1'}, dimensions={0} | all-to-all | bytes 786432 | tf_op jit(solution)/shard_map/all_to_all | solution.py:20
  8.5 0.1 copy.29
  8.7 41.4 %all_to_all.61 = f32[64,6,128]{2,1,0:T(8,128)S(1)} all-to-all(f32[64,6,128]{2,1,0:T(8,128)S(1)} %copy.29), channel_id=1, replica_groups=mesh['delay_0'=4,'delay_1'=8,'row'=4,'col_0'=2,'col_1'=2] {'delay_0','de..., dimensions={0} | all-to-all | bytes 393216 | tf_op jit(solution)/shard_map/all_to_all | solution.py:42
  50.1 0.1 reduce_sum.55
  50.2 26.5 %all_to_all.62 = f32[64,6,128]{2,1,0:T(8,128)S(1)} all-to-all(f32[64,6,128]{2,1,0:T(8,128)S(1)} %broadcast_in_dim.21), channel_id=1, replica_groups=mesh['delay_0'=4,'delay_1'=8,'row'=4,'col_0'=2,'col_1'=2] {'delay_0','de..., dimensions={0} | all-to-all | bytes 393216 | tf_op jit(solution)/shard_map/all_to_all | solution.py:32
  76.8 0.0 copy-start.2
  76.8 4.2 %all_to_all.63 = f32[2,64,6,128]{3,1,2,0:T(8,128)S(1)} all-to-all(f32[2,64,6,128]{3,1,2,0:T(8,128)S(1)} %broadcast_in_dim.22), channel_id=1, replica_groups=mesh['delay_0'=4,'delay_1'=8,'row'=4,'col_0'=2,'col_1'=2] {'col_1'}, dimensions={0} | all-to-all | bytes 786432 | tf_op jit(solution)/shard_map/all_to_all | solution.py:32
  81.0 0.2 copy.31
  81.3 0.0 copy-done
  81.3 0.0 copy-done.2
  81.3 0.5 convolution_bitcast_fusion.2
  81.8 0.9 copy.32
  82.7 0.0 copy-start.1
  82.7 5.0 %all-to-all-start.4 = ((f32[4,192,128]{2,1,0:T(8,128)}), f32[4,192,128]{2,1,0:T(8,128)S(1)}, u32[]{:S(2)}, u32[]{:S(2)}) async-start(f32[4,192,128]{2,1,0:T(8,128)} %bitcast.7), calls=%async_computation.4 | async-start | bytes 786432 | tf_op jit(solution)/shard_map/all_to_all | solution.py:20
  87.7 2.7 %collective-permute-start = (bf16[768,128]{1,0:T(8,128)(2,1)}, bf16[768,128]{1,0:T(8,128)(2,1)S(1)}, u32[]{:S(2)}, u32[]{:S(2)}) collective-permute-start(bf16[768,128]{1,0:T(8,128)(2,1)} %bitcast.1), channel_id=1, source_target_pairs={{0,16},{16,32},{32,48},{48,64},{64,80},{80,96},{96,112},{112,128},... | collective-permute-start | bytes 589832 | tf_op jit(solution)/shard_map/ppermute | solution.py:69
  90.4 4.2 %all-to-all-done.4 = f32[4,192,128]{2,1,0:T(8,128)S(1)} async-done(((f32[4,192,128]{2,1,0:T(8,128)}), f32[4,192,128]{2,1,0:T(8,128)S(1)}, u32[]{:S(2)}, u32[]{:S(2)}) %all-to-all-start.4) | async-done | bytes 393248 | tf_op jit(solution)/shard_map/all_to_all | solution.py:20
  94.6 0.7 broadcast_in_dim.23
  95.3 4.8 %all-to-all-start.5 = ((bf16[4,192,128]{2,1,0:T(8,128)(2,1)}), bf16[4,192,128]{2,1,0:T(8,128)(2,1)S(1)}, u32[]{:S(2)}, u32[]{:S(2)}) async-start(bf16[4,192,128]{2,1,0:T(8,128)(2,1)} %broadcast_in_dim.23), calls=%async_computation.5 | async-start | bytes 393216 | tf_op jit(solution)/shard_map/all_to_all | solution.py:32
  100.1 3.5 %collective-permute-done = bf16[768,128]{1,0:T(8,128)(2,1)S(1)} collective-permute-done((bf16[768,128]{1,0:T(8,128)(2,1)}, bf16[768,128]{1,0:T(8,128)(2,1)S(1)}, u32[]{:S(2)}, u32[]{:S(2)}) %collective-permute-start) | collective-permute-done | bytes 196640 | tf_op jit(solution)/shard_map/ppermute | solution.py:69
  103.7 1.3 all-to-all-done.5
  105.0 0.0 copy-done.1
  105.1 0.5 convolution_bitcast_fusion.1
  105.6 0.2 copy.33
  105.7 0.1 reshape_reshape.11
  105.8 0.1 copy.34
  105.9 4.0 %all_to_all.64 = f32[2,64,6,128]{3,1,2,0:T(8,128)S(1)} all-to-all(f32[2,64,6,128]{3,1,2,0:T(8,128)S(1)} %copy.34), channel_id=1, replica_groups=mesh['delay_0'=4,'delay_1'=8,'row'=4,'col_0'=2,'col_1'=2] {'col_1'}, dimensions={0} | all-to-all | bytes 786432 | tf_op jit(solution)/shard_map/all_to_all | solution.py:20
  110.0 0.1 copy.35
  110.2 30.9 %all_to_all.65 = f32[64,6,128]{2,1,0:T(8,128)S(1)} all-to-all(f32[64,6,128]{2,1,0:T(8,128)S(1)} %copy.35), channel_id=1, replica_groups=mesh['delay_0'=4,'delay_1'=8,'row'=4,'col_0'=2,'col_1'=2] {'delay_0','de..., dimensions={0} | all-to-all | bytes 393216 | tf_op jit(solution)/shard_map/all_to_all | solution.py:42
  141.1 0.1 reduce_sum.58
  141.2 26.5 %all_to_all.66 = f32[64,6,128]{2,1,0:T(8,128)S(1)} all-to-all(f32[64,6,128]{2,1,0:T(8,128)S(1)} %broadcast_in_dim.24), channel_id=1, replica_groups=mesh['delay_0'=4,'delay_1'=8,'row'=4,'col_0'=2,'col_1'=2] {'delay_0','de..., dimensions={0} | all-to-all | bytes 393216 | tf_op jit(solution)/shard_map/all_to_all | solution.py:32
  167.7 4.0 %all_to_all.67 = f32[2,64,6,128]{3,1,2,0:T(8,128)S(1)} all-to-all(f32[2,64,6,128]{3,1,2,0:T(8,128)S(1)} %broadcast_in_dim.25), channel_id=1, replica_groups=mesh['delay_0'=4,'delay_1'=8,'row'=4,'col_0'=2,'col_1'=2] {'col_1'}, dimensions={0} | all-to-all | bytes 786432 | tf_op jit(solution)/shard_map/all_to_all | solution.py:32
  171.8 0.2 copy.37
  172.1 0.5 convolution_bitcast_fusion
  172.6 0.2 copy.38
  172.8 11.0 %all_to_all.68 = f32[4,192,128]{2,1,0:T(8,128)S(1)} all-to-all(f32[4,192,128]{2,1,0:T(8,128)S(1)} %bitcast.50), channel_id=1, replica_groups=mesh['delay_0'=4,'delay_1'=8,'row'=4,'col_0'=2,'col_1'=2] {'row'}, dimensions={0} | all-to-all | bytes 786432 | tf_op jit(solution)/shard_map/all_to_all | solution.py:20
  183.9 0.7 broadcast_in_dim.26
  184.6 4.8 %all-to-all-start.11 = ((bf16[4,192,128]{2,1,0:T(8,128)(2,1)}), bf16[4,192,128]{2,1,0:T(8,128)(2,1)S(1)}, u32[]{:S(2)}, u32[]{:S(2)}) async-start(bf16[4,192,128]{2,1,0:T(8,128)(2,1)} %broadcast_in_dim.26), calls=%async_computation.11 | async-start | bytes 393216 | tf_op jit(solution)/shard_map/all_to_all | solution.py:32
  189.4 2.7 %collective-permute-start.1 = (bf16[768,128]{1,0:T(8,128)(2,1)S(1)}, bf16[768,128]{1,0:T(8,128)(2,1)S(1)}, u32[]{:S(2)}, u32[]{:S(2)}) collective-permute-start(bf16[768,128]{1,0:T(8,128)(2,1)S(1)} %bitcast_select_fusion.1), channel_id=1, source_target_pairs={{0,16},{16,32},{32,48},{48,64},{64,80},{80,96},{96,112},{112,128},... | collective-permute-start | bytes 589832 | tf_op jit(solution)/shard_map/ppermute | solution.py:69
  192.1 2.2 %all-to-all-done.11 = bf16[4,192,128]{2,1,0:T(8,128)(2,1)S(1)} async-done(((bf16[4,192,128]{2,1,0:T(8,128)(2,1)}), bf16[4,192,128]{2,1,0:T(8,128)(2,1)S(1)}, u32[]{:S(2)}, u32[]{:S(2)}) %all-to-all-start.11) | async-done | bytes 196640 | tf_op jit(solution)/shard_map/all_to_all | solution.py:32
  194.2 0.8 pad_maximum_fusion
  195.0 9.5 %collective-permute-done.1 = bf16[768,128]{1,0:T(8,128)(2,1)S(1)} collective-permute-done((bf16[768,128]{1,0:T(8,128)(2,1)S(1)}, bf16[768,128]{1,0:T(8,128)(2,1)S(1)}, u32[]{:S(2)}, u32[]{:S(2)}) %collective-permute-start.1) | collective-permute-done | bytes 196640 | tf_op jit(solution)/shard_map/ppermute | solution.py:69
  204.6 0.7 bitcast_select_fusion
  (13 shorter events, 0.4 us)
Async XLA Ops:
  0.6 80.6 %copy-start = (bf16[768,768]{1,0:T(8,128)(2,1)S(1)}, bf16[768,768]{1,0:T(8,128)(2,1)}, u32[]{:S(2)}) copy-start(bf16[768,768]{1,0:T(8,128)(2,1)} %param.6) | copy-start | bytes 3538948
  76.8 4.5 %copy-start.2 = (bf16[2,768,128]{2,1,0:T(8,128)(2,1)S(1)}, bf16[2,768,128]{2,1,0:T(8,128)(2,1)}, u32[]{:S(2)}) copy-start(bf16[2,768,128]{2,1,0:T(8,128)(2,1)} %param.4) | copy-start | bytes 1179652
  82.7 22.3 %copy-start.1 = (bf16[1,768,768]{2,1,0:T(8,128)(2,1)S(1)}, bf16[1,768,768]{2,1,0:T(8,128)(2,1)}, u32[]{:S(2)}) copy-start(bf16[1,768,768]{2,1,0:T(8,128)(2,1)} %param.5) | copy-start | bytes 3538948
  82.7 11.9 %all-to-all-start.4 = ((f32[4,192,128]{2,1,0:T(8,128)}), f32[4,192,128]{2,1,0:T(8,128)S(1)}, u32[]{:S(2)}, u32[]{:S(2)}) async-start(f32[4,192,128]{2,1,0:T(8,128)} %bitcast.7), calls=%async_computation.4 | async-start | bytes 786432 | tf_op jit(solution)/shard_map/all_to_all | solution.py:20
  87.7 16.0 %collective-permute-start = (bf16[768,128]{1,0:T(8,128)(2,1)}, bf16[768,128]{1,0:T(8,128)(2,1)S(1)}, u32[]{:S(2)}, u32[]{:S(2)}) collective-permute-start(bf16[768,128]{1,0:T(8,128)(2,1)} %bitcast.1), channel_id=1, source_target_pairs={{0,16},{16,32},{32,48},{48,64},{64,80},{80,96},{96,112},{112,128},... | collective-permute-start | bytes 589832 | tf_op jit(solution)/shard_map/ppermute | solution.py:69
  95.3 9.7 %all-to-all-start.5 = ((bf16[4,192,128]{2,1,0:T(8,128)(2,1)}), bf16[4,192,128]{2,1,0:T(8,128)(2,1)S(1)}, u32[]{:S(2)}, u32[]{:S(2)}) async-start(bf16[4,192,128]{2,1,0:T(8,128)(2,1)} %broadcast_in_dim.23), calls=%async_computation.5 | async-start | bytes 393216 | tf_op jit(solution)/shard_map/all_to_all | solution.py:32
  184.6 9.7 %all-to-all-start.11 = ((bf16[4,192,128]{2,1,0:T(8,128)(2,1)}), bf16[4,192,128]{2,1,0:T(8,128)(2,1)S(1)}, u32[]{:S(2)}, u32[]{:S(2)}) async-start(bf16[4,192,128]{2,1,0:T(8,128)(2,1)} %broadcast_in_dim.26), calls=%async_computation.11 | async-start | bytes 393216 | tf_op jit(solution)/shard_map/all_to_all | solution.py:32
  189.4 15.2 %collective-permute-start.1 = (bf16[768,128]{1,0:T(8,128)(2,1)S(1)}, bf16[768,128]{1,0:T(8,128)(2,1)S(1)}, u32[]{:S(2)}, u32[]{:S(2)}) collective-permute-start(bf16[768,128]{1,0:T(8,128)(2,1)S(1)} %bitcast_select_fusion.1), channel_id=1, source_target_pairs={{0,16},{16,32},{32,48},{48,64},{64,80},{80,96},{96,112},{112,128},... | collective-permute-start | bytes 589832 | tf_op jit(solution)/shard_map/ppermute | solution.py:69
where the time goes:
time: 206 us; the launch traced here: 205 us
  blocking collectives  153 us (74%)
  waiting for transfers between devices  20.8 us (10%)
  starting transfers between devices  19.9 us (10%)
  local copies, waits for them, and re-layouts  6.17 us (3%)
  matrix products  3.11 us (2%)
    all_to_all x2, blocking collectives, sum_in_two_steps(): return jnp.sum(lax.all_to_all(own, far, 0, 0, tiled=True), axis=0)  72.3 us
    all_to_all x4, blocking collectives, copy_for_each(): return lax.all_to_all(copies, axis, split_axis=0, concat_axis=0, tiled=True)  61.2 us
    all_to_all x3, blocking collectives, sent_and_summed(): pieces = lax.all_to_all(split_up(shard, dim, count), axis, 0, 0, tiled=True)  19.1 us
    ppermute x2, waiting for transfers between devices, from_behind(): return lax.ppermute(block, axis, route)  13.1 us
    all_to_all x2, starting transfers between devices, copy_for_each(): return lax.all_to_all(copies, axis, split_axis=0, concat_axis=0, tiled=True)  9.59 us
    ppermute x2, starting transfers between devices, from_behind(): return lax.ppermute(block, axis, route)  5.39 us
    all_to_all x1, starting transfers between devices, sent_and_summed(): pieces = lax.all_to_all(split_up(shard, dim, count), axis, 0, 0, tiled=True)  4.95 us
    all_to_all x1, waiting for transfers between devices, sent_and_summed(): pieces = lax.all_to_all(split_up(shard, dim, count), axis, 0, 0, tiled=True)  4.2 us
  transfers between devices with their start and end apart: 5, of which 5 were waited for; matrix products, arithmetic and copies ran while one was open for 1% of the time, Pallas kernels for 0%

commit v1 on v0

v1 whole, which is shorter than its diff:
```python
import jax
import jax.numpy as jnp
from jax import lax
from jax.experimental import pallas as pl
from jax.experimental.pallas import tpu as pltpu
from jax.sharding import PartitionSpec as P

MESH = pl.DeviceIdType.MESH
F32, BF16 = jnp.float32, jnp.bfloat16
STEPS = 2
ROWS = 768
HALF = 384
EXC = 128
NY, NX, NZL, NZ = 4, 4, 8, 16
YE = EXC // NY
XE = YE // NX
NXY = NX * NY


def nt(a, b):
    return lax.dot_general(a, b, (((1,), (1,)), ((), ())), preferred_element_type=F32)


def kernel(exc_in, d_in, inv_in, h_in, cur_out, fin_out,
           exc, dop, inv, hist, hprev, hprev2,
           core_send, core_recv, own_half, y_send, y_recv, z_send, z_recv,
           d0_send, d0_recv, exc_t, rhs, c_own, x_send, x_recv, gath,
           load_sem, h_sem, core_sem, y_ssem, y_rsem, z_ssem, z_rsem,
           d0_ssem, d0_rsem, rhs_sem, x_ssem, x_rsem, b_ssem, b_rsem, g_ssem, g_rsem):
    d = lax.axis_index("delay")
    x = lax.axis_index("row")
    c = lax.axis_index("col")
    y, zl = d // NZL, d % NZL
    zh, k = c // 2, c % 2
    z = zh * NZL + zl
    xy = y * NX + x
    other = 1 - k
    hub = zl == 0
    cell0 = d == 0

    def at(yy, zz, xx, kk):
        return (yy * NZL + zz % NZL, xx, (zz // NZL) * 2 + kk)

    partner = at(y, z, x, other)

    loads = [
        pltpu.make_async_copy(h_in.at[0], hist, load_sem.at[0]),
        pltpu.make_async_copy(d_in.at[0], dop, load_sem.at[1]),
        pltpu.make_async_copy(exc_in, exc, load_sem.at[2]),
        pltpu.make_async_copy(inv_in, inv, load_sem.at[3]),
    ]
    for load in loads:
        load.start()

    barrier = pltpu.get_barrier_semaphore()

    def greet(device):
        pl.semaphore_signal(barrier, inc=1, device_id=device, device_id_type=MESH)

    greet(partner)
    for o in range(1, NXY):
        greet(at((y + o // NX) % NY, z, (x + o % NX) % NX, k))
    for o in range(1, NZ):
        greet(at(y, (z + o) % NZ, x, k))

    @pl.when(hub)
    def _():
        for o in range(1, NY):
            greet(at((y + o) % NY, (z + NZL) % NZ, x, k))

    for step, (low, high) in ((1, (1, NZL - 1)), (2, (2, NZL - 2))):
        @pl.when((zl >= high) & (y < NY - 1))
        def _():
            greet((d + step, x, c))

        @pl.when((zl < low) & (y > 0))
        def _():
            greet((d - step, x, c))

    def one(condition):
        return jnp.where(condition, 1, 0).astype(jnp.int32)

    up, down = y < NY - 1, y > 0
    peers = (
        1 + (NXY - 1) + (NZ - 1) + one(hub) * (NY - 1)
        + one((zl >= NZL - 1) & up) + one((zl < 1) & down)
        + one((zl >= NZL - 2) & up) + one((zl < 2) & down)
    )

    def remote(src, dst, ssem, rsem, device):
        return pltpu.make_async_remote_copy(
            src_ref=src, dst_ref=dst, send_sem=ssem, recv_sem=rsem,
            device_id=device, device_id_type=MESH,
        )

    def partial_sums(i, past):
        away = pl.ds(pl.multiple_of(other * HALF, HALF), HALF)
        mine = pl.ds(pl.multiple_of(k * HALF, HALF), HALF)
        core_send[i] = nt(past, dop[away, :]).astype(BF16)
        return mine

    def core_copy(i):
        return remote(core_send.at[i], core_recv.at[i], core_sem.at[i, 0], core_sem.at[i, 1], partner)

    def y_copy(s, o):
        peer = (y + o) % NY
        return remote(y_send.at[s, peer], y_recv.at[s, o - 1], y_ssem.at[s, o - 1],
                      y_rsem.at[s, o - 1], at(peer, z, x, k))

    def z_copy(s, hh):
        return remote(z_send.at[s], z_recv.at[s, z], z_ssem.at[s, hh], z_rsem.at[s, z],
                      at(y, hh * NZL, x, k))

    def y_stage(s):
        core_copy(s).wait_recv()
        total = own_half[s] + core_recv[s].astype(F32)
        y_send[s] = total.astype(BF16).reshape(NY, YE, HALF)
        for o in range(1, NY):
            y_copy(s, o).start()

    def z_stage(s):
        for o in range(1, NY):
            y_copy(s, o).wait_recv()
        total = y_send[s, y].astype(F32)
        for o in range(NY - 1):
            total = total + y_recv[s, o].astype(F32)
        z_send[s] = total.astype(BF16)
        for hh in range(2):
            @pl.when(z != hh * NZL)
            def _():
                z_copy(s, hh).start()

    h_copies = [
        remote(hist, hprev, h_sem.at[0], h_sem.at[1], (jnp.minimum(d + 1, 31), x, c)),
        remote(hist, hprev2, h_sem.at[2], h_sem.at[3], (jnp.minimum(d + 2, 31), x, c)),
    ]

    loads[0].wait()
    loads[1].wait()
    past = hist[...].astype(F32).T.astype(BF16)
    mine = partial_sums(0, past)
    pl.semaphore_wait(barrier, peers)
    core_copy(0).start()

    @pl.when(d < 31)
    def _():
        h_copies[0].start()

    own_half[0] = nt(past, dop[mine, :])
    y_stage(0)

    loads[2].wait()
    loads[3].wait()

    @pl.when(hub)
    def _():
        rows = pl.ds(pl.multiple_of(k * HALF, HALF), HALF)
        for s in range(STEPS):
            exc_t[s] = exc[s, rows, :].astype(F32).T.reshape(NY, YE, HALF)

    z_stage(0)

    @pl.when(d > 0)
    def _():
        h_copies[0].wait_recv()

    @pl.when(d == 0)
    def _():
        hprev[...] = jnp.zeros_like(hprev)

    past = hprev[...].astype(F32).T.astype(BF16)
    mine = partial_sums(1, past)
    core_copy(1).start()
    own_half[1] = nt(past, dop[mine, :])
    y_stage(1)
    z_stage(1)

    @pl.when(d < 30)
    def _():
        h_copies[1].start()

    def rhs_copy(s):
        return remote(rhs.at[s, k], rhs.at[s, k], rhs_sem.at[s, 0], rhs_sem.at[s, 1], partner)

    def rhs_arrival(s):
        return remote(rhs.at[s, other], rhs.at[s, other], rhs_sem.at[s, 0], rhs_sem.at[s, 1], partner)

    def x_copy(s, o):
        peer = (x + o) % NX
        return remote(x_send.at[s, peer], x_recv.at[s, o - 1], x_ssem.at[s, o - 1],
                      x_rsem.at[s, o - 1], at(y, z, peer, k))

    def b_copy(s, zz):
        return remote(gath.at[s, xy], gath.at[s, xy], b_ssem.at[s, zz - 1], b_rsem.at[s],
                      at(y, zh * NZL + zz, x, k))

    def g_copy(s, o):
        py, px = (y + o // NX) % NY, (x + o % NX) % NX
        return remote(gath.at[s, xy], gath.at[s, xy], g_ssem.at[s, o - 1], g_rsem.at[s, o - 1],
                      at(py, z, px, k))

    def g_arrival(s, o):
        py, px = (y + NY - o // NX) % NY, (x + NX - o % NX) % NX
        there = py * NX + px
        return remote(gath.at[s, there], gath.at[s, there], g_ssem.at[s, o - 1], g_rsem.at[s, o - 1],
                      at(py, z, px, k))

    def hub_step(s):
        total = exc_t[s, y] - z_send[s].astype(F32)
        for o in range(1, NZ):
            far = (z + o) % NZ
            remote(z_recv.at[s, far], z_recv.at[s, far], z_ssem.at[s, 0], z_rsem.at[s, far],
                   partner).wait_recv()
            total = total - z_recv[s, far].astype(F32)
        if s == 1:
            for hh in range(2):
                @pl.when(jnp.logical_not(cell0 & (zh == hh)))
                def _():
                    remote(d0_recv.at[hh], d0_recv.at[hh], d0_ssem.at[0], d0_rsem.at[hh],
                           partner).wait_recv()
            total = total - d0_recv[0].astype(F32) - d0_recv[1].astype(F32)
        rhs[s, k] = total.astype(BF16)
        rhs_copy(s).start()
        rhs_arrival(s).wait_recv()
        product = nt(rhs[s, 0], inv[:, :HALF]) + nt(rhs[s, 1], inv[:, HALF:])
        product = product.reshape(NX, XE, ROWS)
        c_own[...] = product
        x_send[s] = product.astype(BF16)
        for o in range(1, NX):
            x_copy(s, o).start()
        total = c_own[x]
        for o in range(1, NX):
            x_copy(s, o).wait_recv()
            total = total + x_recv[s, o - 1].astype(F32)
        gath[s, xy] = total.astype(BF16)
        if s == 1:
            for zz in range(NZL - 1, 0, -1):
                b_copy(s, zz).start()
        for o in range(1, NXY):
            g_copy(s, o).start()
        if s == 0:
            for zz in range(NZL - 1, 0, -1):
                b_copy(s, zz).start()

    def relay(s):
        b_copy(s, 1).wait_recv()
        for o in range(1, NXY):
            g_copy(s, o).start()

    def gathered(s):
        for o in range(1, NXY):
            g_arrival(s, o).wait_recv()

    def whole(s):
        return gath[s].astype(F32).reshape(EXC, ROWS)

    def d0_copy(o, hh):
        peer = (y + o) % NY
        return remote(d0_send.at[peer], d0_recv.at[zh], d0_ssem.at[o * 2 + hh], d0_rsem.at[zh],
                      at(peer, hh * NZL, x, k))

    @pl.when(hub)
    def _():
        hub_step(0)

    @pl.when(cell0)
    def _():
        gathered(0)
        mine = partial_sums(2, whole(0).astype(BF16))
        core_copy(2).start()
        own_half[0] = nt(whole(0).astype(BF16), dop[mine, :])
        core_copy(2).wait_recv()
        total = (own_half[0] + core_recv[2].astype(F32)).astype(BF16)
        d0_send[...] = total.reshape(NY, YE, HALF)
        d0_recv[zh] = d0_send[y]
        for hh in range(2):
            for o in range(NY):
                if o == 0:
                    @pl.when(zh != hh)
                    def _():
                        d0_copy(o, hh).start()
                else:
                    d0_copy(o, hh).start()

    @pl.when(hub)
    def _():
        hub_step(1)

    @pl.when(jnp.logical_not(hub))
    def _():
        relay(0)

    @pl.when(jnp.logical_not(cell0))
    def _():
        gathered(0)

    cur_out[0] = whole(0).T.astype(BF16)

    @pl.when(d == 1)
    def _():
        fin_out[0] = cur_out[0]

    @pl.when(d > 1)
    def _():
        h_copies[1].wait_recv()
        fin_out[0] = hprev2[...]

    @pl.when(jnp.logical_not(hub))
    def _():
        relay(1)

    gathered(1)
    cur_out[1] = whole(1).T.astype(BF16)

    @pl.when(d == 0)
    def _():
        fin_out[0] = cur_out[1]

    @pl.when(d < 31)
    def _():
        h_copies[0].wait_send()

    @pl.when(d < 30)
    def _():
        h_copies[1].wait_send()

    for s in range(STEPS):
        core_copy(s).wait_send()
        for o in range(1, NY):
            y_copy(s, o).wait_send()
        for hh in range(2):
            @pl.when(z != hh * NZL)
            def _():
                z_copy(s, hh).wait_send()
        for o in range(1, NXY):
            g_copy(s, o).wait_send()

    @pl.when(hub)
    def _():
        for s in range(STEPS):
            rhs_copy(s).wait_send()
            for o in range(1, NX):
                x_copy(s, o).wait_send()
            for zz in range(1, NZL):
                b_copy(s, zz).wait_send()

    @pl.when(cell0)
    def _():
        core_copy(2).wait_send()
        for hh in range(2):
            for o in range(NY):
                if o == 0:
                    @pl.when(zh != hh)
                    def _():
                        d0_copy(o, hh).wait_send()
                else:
                    d0_copy(o, hh).wait_send()


def on_device(excitation, delay_ops, inverse_op, history):
    vmem, dma = pltpu.VMEM, pltpu.SemaphoreType.DMA
    return pl.pallas_call(
        kernel,
        out_shape=(
            jax.ShapeDtypeStruct((STEPS, ROWS, EXC), BF16),
            jax.ShapeDtypeStruct((1, ROWS, EXC), BF16),
        ),
        in_specs=[pl.BlockSpec(memory_space=pl.ANY)] * 4,
        out_specs=(pl.BlockSpec(memory_space=pltpu.VMEM),) * 2,
        scratch_shapes=[
            vmem((STEPS, ROWS, EXC), BF16),
            vmem((ROWS, ROWS), BF16),
            vmem((ROWS, ROWS), BF16),
            vmem((ROWS, EXC), BF16),
            vmem((ROWS, EXC), BF16),
            vmem((ROWS, EXC), BF16),
            vmem((3, EXC, HALF), BF16),
            vmem((3, EXC, HALF), BF16),
            vmem((STEPS, EXC, HALF), F32),
            vmem((STEPS, NY, YE, HALF), BF16),
            vmem((STEPS, NY - 1, YE, HALF), BF16),
            vmem((STEPS, YE, HALF), BF16),
            vmem((STEPS, NZ, YE, HALF), BF16),
            vmem((NY, YE, HALF), BF16),
            vmem((2, YE, HALF), BF16),
            vmem((STEPS, NY, YE, HALF), F32),
            vmem((STEPS, 2, YE, HALF), BF16),
            vmem((NX, XE, ROWS), F32),
            vmem((STEPS, NX, XE, ROWS), BF16),
            vmem((STEPS, NX - 1, XE, ROWS), BF16),
            vmem((STEPS, NXY, XE, ROWS), BF16),
            dma((4,)),
            dma((4,)),
            dma((3, 2)),
            dma((STEPS, NY - 1)),
            dma((STEPS, NY - 1)),
            dma((STEPS, 2)),
            dma((STEPS, NZ)),
            dma((8,)),
            dma((2,)),
            dma((STEPS, 2)),
            dma((STEPS, NX - 1)),
            dma((STEPS, NX - 1)),
            dma((STEPS, NZL - 1)),
            dma((STEPS,)),
            dma((STEPS, NXY - 1)),
            dma((STEPS, NXY - 1)),
        ],
        compiler_params=pltpu.CompilerParams(collective_id=0, has_side_effects=True),
    )(excitation, delay_ops, inverse_op, history)


def solution(mesh):
    in_specs = (
        P(None, "row", None), P("delay", "row", "col"), P("col", "row"), P("delay", "col", None),
    )
    out_specs = (P(None, "col", None), P("delay", "col", None))
    return jax.shard_map(
        on_device, mesh=mesh, in_specs=in_specs, out_specs=out_specs, check_vma=False
    )
```

time: 206 us -> 79.5 us (0.39)
  the two profiles are of different devices: /device:TPU:10 before, /device:TPU:32 now
where the time goes in v1:
time: 79.5 us; the launch traced here: 79.3 us
  Pallas kernels  75.3 us (95%)
  local copies, waits for them, and re-layouts  3.38 us (4%)
    pallas_call x1, Pallas kernels, on_device(): pl.pallas_call(kernel, out_shape=(jax.ShapeDtypeStruct((STEPS, ROWS, EXC)...  75.3 us
    unnamed x2, local copies, waits for them, and re-layouts  3.38 us

profile of v1, /device:TPU:32, one launch (start us, length us, event | category | flops | bytes accessed | tf_op | source)
XLA Modules:
  0.0 79.3 jit_solution(7068466191024244090)
XLA Ops:
  0.6 75.3 %shard_map.59 = (bf16[2,768,128]{2,1,0:T(8,128)(2,1)}, bf16[1,768,128]{2,1,0:T(8,128)(2,1)}) custom-call(bf16[2,768,128]{2,1,0:T(8,128)(2,1)} %exc_in.1, bf16[1,768,768]{2,1,0:T(8,128)(2,1)} %d_in.1, bf16[768,768]{1,0:T(8,128)(2,1)} %inv_in.1, bf16[1,768,128]{2,1,0:T(8,128)(2,1)} %h_in.1), custom_call_target="tpu_custom_call" | custom-call | tf_op jit(solution)/shard_map/pallas_call | solution.py:362
  75.9 1.8 %copy.8 = bf16[2,768,128]{2,1,0:T(8,128)(2,1)} copy(bf16[2,768,128]{2,1,0:T(8,128)(2,1)} %get-tuple-element.4) | data formatting | bytes 786432
  77.7 1.6 %copy.9 = bf16[1,768,128]{2,1,0:T(8,128)(2,1)} copy(bf16[1,768,128]{2,1,0:T(8,128)(2,1)} %get-tuple-element.5) | data formatting | bytes 393216

commit v2 on v1

--- a/solution.py
+++ b/solution.py
@@ -11,9 +11,11 @@
 ROWS = 768
 HALF = 384
 EXC = 128
+LANES = 128
 NY, NX, NZL, NZ = 4, 4, 8, 16
 YE = EXC // NY
 XE = YE // NX
+QUART = ROWS // NX
 NXY = NX * NY
 
 
@@ -22,10 +24,10 @@
 
 
 def kernel(exc_in, d_in, inv_in, h_in, cur_out, fin_out,
-           exc, dop, inv, hist, hprev, hprev2,
+           exc, dop, inv, hist, older,
            core_send, core_recv, own_half, y_send, y_recv, z_send, z_recv,
            d0_send, d0_recv, exc_t, rhs, c_own, x_send, x_recv, gath,
-           load_sem, h_sem, core_sem, y_ssem, y_rsem, z_ssem, z_rsem,
+           load_sem, d_sem, h_sem, hx_ssem, hx_rsem, core_sem, y_ssem, y_rsem, z_ssem, z_rsem,
            d0_ssem, d0_rsem, rhs_sem, x_ssem, x_rsem, b_ssem, b_rsem, g_ssem, g_rsem):
     d = lax.axis_index("delay")
     x = lax.axis_index("row")
@@ -43,14 +45,18 @@
 
     partner = at(y, z, x, other)
 
+    def d_load(i):
+        part = pl.ds(pl.multiple_of(lax.rem(other * 3 + i, 6) * LANES, LANES), LANES)
+        return pltpu.make_async_copy(d_in.at[0, part], dop.at[part], d_sem.at[i])
+
     loads = [
         pltpu.make_async_copy(h_in.at[0], hist, load_sem.at[0]),
-        pltpu.make_async_copy(d_in.at[0], dop, load_sem.at[1]),
-        pltpu.make_async_copy(exc_in, exc, load_sem.at[2]),
-        pltpu.make_async_copy(inv_in, inv, load_sem.at[3]),
+        pltpu.make_async_copy(exc_in, exc, load_sem.at[1]),
+        pltpu.make_async_copy(inv_in, inv, load_sem.at[2]),
     ]
-    for load in loads:
-        load.start()
+    loads[0].start()
+    for i in range(6):
+        d_load(i).start()
 
     barrier = pltpu.get_barrier_semaphore()
 
@@ -58,34 +64,28 @@
         pl.semaphore_signal(barrier, inc=1, device_id=device, device_id_type=MESH)
 
     greet(partner)
-    for o in range(1, NXY):
-        greet(at((y + o // NX) % NY, z, (x + o % NX) % NX, k))
-    for o in range(1, NZ):
-        greet(at(y, (z + o) % NZ, x, k))
+    for o in range(1, NY):
+        greet(at((y + o) % NY, z, x, k))
+    for o in range(1, NX):
+        greet(at(y, z, (x + o) % NX, k))
 
     @pl.when(hub)
     def _():
-        for o in range(1, NY):
-            greet(at((y + o) % NY, (z + NZL) % NZ, x, k))
-
-    for step, (low, high) in ((1, (1, NZL - 1)), (2, (2, NZL - 2))):
-        @pl.when((zl >= high) & (y < NY - 1))
-        def _():
-            greet((d + step, x, c))
-
-        @pl.when((zl < low) & (y > 0))
-        def _():
-            greet((d - step, x, c))
+        for o in range(1, NZ):
+            greet(at(y, (z + o) % NZ, x, k))
+
+    @pl.when(d > 0)
+    def _():
+        greet((d - 1, x, c))
+
+    @pl.when(d > 1)
+    def _():
+        greet((d - 2, x, c))
 
     def one(condition):
         return jnp.where(condition, 1, 0).astype(jnp.int32)
 
-    up, down = y < NY - 1, y > 0
-    peers = (
-        1 + (NXY - 1) + (NZ - 1) + one(hub) * (NY - 1)
-        + one((zl >= NZL - 1) & up) + one((zl < 1) & down)
-        + one((zl >= NZL - 2) & up) + one((zl < 2) & down)
-    )
+    peers = 1 + (NY - 1) + (NX - 1) + 2 - one(hub) + one(d < 31) + one(d < 30)
 
     def remote(src, dst, ssem, rsem, device):
         return pltpu.make_async_remote_copy(
@@ -130,27 +130,50 @@
             def _():
                 z_copy(s, hh).start()
 
-    h_copies = [
-        remote(hist, hprev, h_sem.at[0], h_sem.at[1], (jnp.minimum(d + 1, 31), x, c)),
-        remote(hist, hprev2, h_sem.at[2], h_sem.at[3], (jnp.minimum(d + 2, 31), x, c)),
-    ]
+    quarter = pl.ds(pl.multiple_of(x * QUART, QUART), QUART)
+
+    def h_copy(i):
+        return remote(hist.at[quarter], older.at[i, quarter], h_sem.at[i, 0], h_sem.at[i, 1],
+                      (jnp.minimum(d + 1 + i, 31), x, c))
+
+    def hx_copy(i, o):
+        return remote(older.at[i, quarter], older.at[i, quarter], hx_ssem.at[i, o - 1],
+                      hx_rsem.at[i, o - 1], at(y, z, (x + o) % NX, k))
+
+    def hx_arrival(i, o):
+        theirs = pl.ds(pl.multiple_of((x + NX - o) % NX * QUART, QUART), QUART)
+        return remote(older.at[i, theirs], older.at[i, theirs], hx_ssem.at[i, o - 1],
+                      hx_rsem.at[i, o - 1], partner)
+
+    def h_pass(i):
+        h_copy(i).wait_recv()
+        for o in range(1, NX):
+            hx_copy(i, o).start()
+
+    def h_whole(i):
+        for o in range(1, NX):
+            hx_arrival(i, o).wait_recv()
 
     loads[0].wait()
-    loads[1].wait()
     past = hist[...].astype(F32).T.astype(BF16)
+    for i in range(3):
+        d_load(i).wait()
+    loads[1].start()
+    loads[2].start()
     mine = partial_sums(0, past)
     pl.semaphore_wait(barrier, peers)
     core_copy(0).start()
 
     @pl.when(d < 31)
     def _():
-        h_copies[0].start()
-
+        h_copy(0).start()
+
+    for i in range(3, 6):
+        d_load(i).wait()
     own_half[0] = nt(past, dop[mine, :])
     y_stage(0)
-
+    loads[1].wait()
     loads[2].wait()
-    loads[3].wait()
 
     @pl.when(hub)
     def _():
@@ -160,24 +183,11 @@
 
     z_stage(0)
 
-    @pl.when(d > 0)
-    def _():
-        h_copies[0].wait_recv()
-
-    @pl.when(d == 0)
-    def _():
-        hprev[...] = jnp.zeros_like(hprev)
-
-    past = hprev[...].astype(F32).T.astype(BF16)
-    mine = partial_sums(1, past)
-    core_copy(1).start()
-    own_half[1] = nt(past, dop[mine, :])
-    y_stage(1)
-    z_stage(1)
-
-    @pl.when(d < 30)
-    def _():
-        h_copies[1].start()
+    @pl.when(cell0)
+    def _():
+        y_send[1] = jnp.zeros_like(y_send[1])
+        for o in range(1, NY):
+            y_copy(1, o).start()
 
     def rhs_copy(s):
         return remote(rhs.at[s, k], rhs.at[s, k], rhs_sem.at[s, 0], rhs_sem.at[s, 1], partner)
@@ -228,6 +238,10 @@
         x_send[s] = product.astype(BF16)
         for o in range(1, NX):
             x_copy(s, o).start()
+        if s == 0:
+            @pl.when(jnp.logical_not(cell0))
+            def _():
+                h_pass(0)
         total = c_own[x]
         for o in range(1, NX):
             x_copy(s, o).wait_recv()
@@ -236,8 +250,12 @@
         if s == 1:
             for zz in range(NZL - 1, 0, -1):
                 b_copy(s, zz).start()
-        for o in range(1, NXY):
-            g_copy(s, o).start()
+        for j in range(NY):
+            oy = (NY - y + j) % NY
+            for ox in range(NX):
+                @pl.when((oy != 0) | (ox != 0))
+                def _():
+                    g_copy(s, oy * NX + ox).start()
         if s == 0:
             for zz in range(NZL - 1, 0, -1):
                 b_copy(s, zz).start()
@@ -273,14 +291,29 @@
         total = (own_half[0] + core_recv[2].astype(F32)).astype(BF16)
         d0_send[...] = total.reshape(NY, YE, HALF)
         d0_recv[zh] = d0_send[y]
-        for hh in range(2):
-            for o in range(NY):
-                if o == 0:
-                    @pl.when(zh != hh)
-                    def _():
-                        d0_copy(o, hh).start()
-                else:
-                    d0_copy(o, hh).start()
+        for o in (2, 1, 3, 0):
+            d0_copy(o, 1 - zh).start()
+        for o in range(1, NY):
+            d0_copy(o, zh).start()
+
+    @pl.when(jnp.logical_not(cell0))
+    def _():
+        @pl.when(jnp.logical_not(hub))
+        def _():
+            h_pass(0)
+
+        h_whole(0)
+        past = older[0].astype(F32).T.astype(BF16)
+        mine = partial_sums(1, past)
+        core_copy(1).start()
+        own_half[1] = nt(past, dop[mine, :])
+        y_stage(1)
+
+    z_stage(1)
+
+    @pl.when(d < 30)
+    def _():
+        h_copy(1).start()
 
     @pl.when(hub)
     def _():
@@ -294,6 +327,10 @@
     def _():
         gathered(0)
 
+    @pl.when(d > 1)
+    def _():
+        h_pass(1)
+
     cur_out[0] = whole(0).T.astype(BF16)
 
     @pl.when(d == 1)
@@ -302,8 +339,8 @@
 
     @pl.when(d > 1)
     def _():
-        h_copies[1].wait_recv()
-        fin_out[0] = hprev2[...]
+        h_whole(1)
+        fin_out[0] = older[1]
 
     @pl.when(jnp.logical_not(hub))
     def _():
@@ -316,16 +353,23 @@
     def _():
         fin_out[0] = cur_out[1]
 
-    @pl.when(d < 31)
-    def _():
-        h_copies[0].wait_send()
-
-    @pl.when(d < 30)
-    def _():
-        h_copies[1].wait_send()
+    for i in range(2):
+        @pl.when(d < 31 - i)
+        def _():
+            h_copy(i).wait_send()
+
+        @pl.when(d > i)
+        def _():
+            for o in range(1, NX):
+                hx_copy(i, o).wait_send()
+
+    core_copy(0).wait_send()
+
+    @pl.when(jnp.logical_not(cell0))
+    def _():
+        core_copy(1).wait_send()
 
     for s in range(STEPS):
-        core_copy(s).wait_send()
         for o in range(1, NY):
             y_copy(s, o).wait_send()
         for hh in range(2):
@@ -347,24 +391,28 @@
     @pl.when(cell0)
     def _():
         core_copy(2).wait_send()
-        for hh in range(2):
-            for o in range(NY):
-                if o == 0:
-                    @pl.when(zh != hh)
-                    def _():
-                        d0_copy(o, hh).wait_send()
-                else:
-                    d0_copy(o, hh).wait_send()
+        for o in range(NY):
+            d0_copy(o, 1 - zh).wait_send()
+        for o in range(1, NY):
+            d0_copy(o, zh).wait_send()
+
+
+def store(cur, fin, cur_out, fin_out, sem):
+    copies = [
+        pltpu.make_async_copy(cur, cur_out, sem.at[0]),
+        pltpu.make_async_copy(fin, fin_out, sem.at[1]),
+    ]
+    for copy in copies:
+        copy.start()
+    for copy in copies:
+        copy.wait()
 
 
 def on_device(excitation, delay_ops, inverse_op, history):
     vmem, dma = pltpu.VMEM, pltpu.SemaphoreType.DMA
-    return pl.pallas_call(
+    results = pl.pallas_call(
         kernel,
-        out_shape=(
-            jax.ShapeDtypeStruct((STEPS, ROWS, EXC), BF16),
-            jax.ShapeDtypeStruct((1, ROWS, EXC), BF16),
-        ),
+        out_shape=(vmem((STEPS, ROWS, EXC), BF16), vmem((1, ROWS, EXC), BF16)),
         in_specs=[pl.BlockSpec(memory_space=pl.ANY)] * 4,
         out_specs=(pl.BlockSpec(memory_space=pltpu.VMEM),) * 2,
         scratch_shapes=[
@@ -372,8 +420,7 @@
             vmem((ROWS, ROWS), BF16),
             vmem((ROWS, ROWS), BF16),
             vmem((ROWS, EXC), BF16),
-            vmem((ROWS, EXC), BF16),
-            vmem((ROWS, EXC), BF16),
+            vmem((2, ROWS, EXC), BF16),
             vmem((3, EXC, HALF), BF16),
             vmem((3, EXC, HALF), BF16),
             vmem((STEPS, EXC, HALF), F32),
@@ -389,8 +436,11 @@
             vmem((STEPS, NX, XE, ROWS), BF16),
             vmem((STEPS, NX - 1, XE, ROWS), BF16),
             vmem((STEPS, NXY, XE, ROWS), BF16),
-            dma((4,)),
-            dma((4,)),
+            dma((3,)),
+            dma((6,)),
+            dma((2, 2)),
+            dma((2, NX - 1)),
+            dma((2, NX - 1)),
             dma((3, 2)),
             dma((STEPS, NY - 1)),
             dma((STEPS, NY - 1)),
@@ -408,6 +458,16 @@
         ],
         compiler_params=pltpu.CompilerParams(collective_id=0, has_side_effects=True),
     )(excitation, delay_ops, inverse_op, history)
+    return pl.pallas_call(
+        store,
+        out_shape=(
+            jax.ShapeDtypeStruct((STEPS, ROWS, EXC), BF16),
+            jax.ShapeDtypeStruct((1, ROWS, EXC), BF16),
+        ),
+        in_specs=[pl.BlockSpec(memory_space=pltpu.VMEM)] * 2,
+        out_specs=(pl.BlockSpec(memory_space=pl.ANY),) * 2,
+        scratch_shapes=[dma((2,))],
+    )(*[pltpu.with_memory_space_constraint(r, pltpu.VMEM) for r in results])
 
 
 def solution(mesh):

time: 79.5 us -> 64.3 us (0.81)
  Pallas kernels: 75.3 us -> 63.5 us
  local copies, waits for them, and re-layouts: 3.38 us -> 0 us
    pallas_call x1 -> x2, Pallas kernels: 75.3 us -> 63.5 us  [the longest x1 62.7 us: on_device(): pl.pallas_call(kernel, out_shape=(vmem((STEPS, ROWS, EXC), BF16), vmem((1...]
    unnamed x2 -> x0, local copies, waits for them, and re-layouts: 3.38 us -> none
where the time goes in v2:
time: 64.3 us; the launch traced here: 64.2 us
  Pallas kernels  63.5 us (99%)
    pallas_call x1, Pallas kernels, on_device(): pl.pallas_call(kernel, out_shape=(vmem((STEPS, ROWS, EXC), BF16), vmem((1...  62.7 us

profile of v2, /device:TPU:32, one launch (start us, length us, event | category | flops | bytes accessed | tf_op | source)
XLA Modules:
  0.0 64.2 jit_solution(377008296548412761)
XLA Ops:
  0.6 62.7 %shard_map.59 = (bf16[2,768,128]{2,1,0:T(8,128)(2,1)S(1)}, bf16[1,768,128]{2,1,0:T(8,128)(2,1)S(1)}) custom-call(bf16[2,768,128]{2,1,0:T(8,128)(2,1)} %exc_in.1, bf16[1,768,768]{2,1,0:T(8,128)(2,1)} %d_in.1, bf16[768,768]{1,0:T(8,128)(2,1)} %inv_in.1, bf16[1,768,128]{2,1,0:T(8,128)(2,1)} %h_in.1), custom_call_target="tpu_custom_call" | custom-call | tf_op jit(solution)/shard_map/pallas_call | solution.py:413
  63.3 0.8 %shard_map.60 = (bf16[2,768,128]{2,1,0:T(8,128)(2,1)}, bf16[1,768,128]{2,1,0:T(8,128)(2,1)}) custom-call(bf16[2,768,128]{2,1,0:T(8,128)(2,1)S(1)} %get-tuple-element.4.cur, bf16[1,768,128]{2,1,0:T(8,128)(2,1)S(1)} %get-tuple-element.5.fin), custom_call_target="tpu_custom_call" | custom-call | tf_op jit(solution)/shard_map/pallas_call | solution.py:461

commit v3 on v2

--- a/solution.py
+++ b/solution.py
@@ -28,7 +28,7 @@
            core_send, core_recv, own_half, y_send, y_recv, z_send, z_recv,
            d0_send, d0_recv, exc_t, rhs, c_own, x_send, x_recv, gath,
            load_sem, d_sem, h_sem, hx_ssem, hx_rsem, core_sem, y_ssem, y_rsem, z_ssem, z_rsem,
-           d0_ssem, d0_rsem, rhs_sem, x_ssem, x_rsem, b_ssem, b_rsem, g_ssem, g_rsem):
+           d0_ssem, d0_rsem, rhs_sem, x_ssem, x_rsem, b_ssem, b_rsem, g_ssem, g_rsem, far_sem):
     d = lax.axis_index("delay")
     x = lax.axis_index("row")
     c = lax.axis_index("col")
@@ -47,6 +47,10 @@
 
     def d_load(i):
         part = pl.ds(pl.multiple_of(lax.rem(other * 3 + i, 6) * LANES, LANES), LANES)
+        return pltpu.make_async_copy(d_in.at[0, part], dop.at[part], d_sem.at[i // 3])
+
+    def d_half(i, which):
+        part = pl.ds(pl.multiple_of(which * HALF, HALF), HALF)
         return pltpu.make_async_copy(d_in.at[0, part], dop.at[part], d_sem.at[i])
 
     loads = [
@@ -71,8 +75,19 @@
 
     @pl.when(hub)
     def _():
-        for o in range(1, NZ):
-            greet(at(y, (z + o) % NZ, x, k))
+        for zz in range(NZL, NZ):
+            @pl.when(z != zz)
+            def _():
+                greet(at(y, zz, x, k))
+
+    @pl.when(z == 0)
+    def _():
+        for zz in range(1, NZL):
+            greet(at(y, zz, x, k))
+
+    @pl.when((zh == 0) & (zl > 0))
+    def _():
+        greet(at(y, NZL, x, k))
 
     @pl.when(d > 0)
     def _():
@@ -85,7 +100,10 @@
     def one(condition):
         return jnp.where(condition, 1, 0).astype(jnp.int32)
 
-    peers = 1 + (NY - 1) + (NX - 1) + 2 - one(hub) + one(d < 31) + one(d < 30)
+    peers = (
+        1 + (NY - 1) + (NX - 1) + one(d < 31) + one(d < 30)
+        + one(z > 0) + one(z > NZL) + one(z == NZL) * (NZL - 1)
+    )
 
     def remote(src, dst, ssem, rsem, device):
         return pltpu.make_async_remote_copy(
@@ -104,11 +122,17 @@
 
     def y_copy(s, o):
         peer = (y + o) % NY
-        return remote(y_send.at[s, peer], y_recv.at[s, o - 1], y_ssem.at[s, o - 1],
-                      y_rsem.at[s, o - 1], at(peer, z, x, k))
+        return remote(y_send.at[s, peer], y_recv.at[s, o - 1], y_ssem.at[s], y_rsem.at[s],
+                      at(peer, z, x, k))
+
+    def all_of(ref, ssem, rsem):
+        return remote(ref, ref, ssem, rsem, partner)
+
+    def y_all(s):
+        return all_of(y_recv.at[s], y_ssem.at[s], y_rsem.at[s])
 
     def z_copy(s, hh):
-        return remote(z_send.at[s], z_recv.at[s, z], z_ssem.at[s, hh], z_rsem.at[s, z],
+        return remote(z_send.at[s], z_recv.at[s, z], z_ssem.at[s, hh], z_rsem.at[s],
                       at(y, hh * NZL, x, k))
 
     def y_stage(s):
@@ -119,13 +143,17 @@
             y_copy(s, o).start()
 
     def z_stage(s):
-        for o in range(1, NY):
-            y_copy(s, o).wait_recv()
+        y_all(s).wait_recv()
         total = y_send[s, y].astype(F32)
         for o in range(NY - 1):
             total = total + y_recv[s, o].astype(F32)
         z_send[s] = total.astype(BF16)
         for hh in range(2):
+            if s == 0 and hh == 1:
+                @pl.when(zh == 0)
+                def _():
+                    pl.semaphore_wait(far_sem, 1)
+
             @pl.when(z != hh * NZL)
             def _():
                 z_copy(s, hh).start()
@@ -137,13 +165,11 @@
                       (jnp.minimum(d + 1 + i, 31), x, c))
 
     def hx_copy(i, o):
-        return remote(older.at[i, quarter], older.at[i, quarter], hx_ssem.at[i, o - 1],
-                      hx_rsem.at[i, o - 1], at(y, z, (x + o) % NX, k))
-
-    def hx_arrival(i, o):
-        theirs = pl.ds(pl.multiple_of((x + NX - o) % NX * QUART, QUART), QUART)
-        return remote(older.at[i, theirs], older.at[i, theirs], hx_ssem.at[i, o - 1],
-                      hx_rsem.at[i, o - 1], partner)
+        return remote(older.at[i, quarter], older.at[i, quarter], hx_ssem.at[i], hx_rsem.at[i],
+                      at(y, z, (x + o) % NX, k))
+
+    def hx_all(i):
+        return all_of(older.at[i, pl.ds(0, ROWS - QUART)], hx_ssem.at[i], hx_rsem.at[i])
 
     def h_pass(i):
         h_copy(i).wait_recv()
@@ -151,25 +177,28 @@
             hx_copy(i, o).start()
 
     def h_whole(i):
-        for o in range(1, NX):
-            hx_arrival(i, o).wait_recv()
+        hx_all(i).wait_recv()
 
     loads[0].wait()
     past = hist[...].astype(F32).T.astype(BF16)
-    for i in range(3):
-        d_load(i).wait()
+    d_half(0, other).wait()
     loads[1].start()
     loads[2].start()
     mine = partial_sums(0, past)
     pl.semaphore_wait(barrier, peers)
+
+    @pl.when(z == NZL)
+    def _():
+        for zz in range(NZL):
+            pl.semaphore_signal(far_sem, inc=1, device_id=at(y, zz, x, k), device_id_type=MESH)
+
     core_copy(0).start()
 
     @pl.when(d < 31)
     def _():
         h_copy(0).start()
 
-    for i in range(3, 6):
-        d_load(i).wait()
+    d_half(1, k).wait()
     own_half[0] = nt(past, dop[mine, :])
     y_stage(0)
     loads[1].wait()
@@ -197,37 +226,38 @@
 
     def x_copy(s, o):
         peer = (x + o) % NX
-        return remote(x_send.at[s, peer], x_recv.at[s, o - 1], x_ssem.at[s, o - 1],
-                      x_rsem.at[s, o - 1], at(y, z, peer, k))
+        return remote(x_send.at[s, peer], x_recv.at[s, o - 1], x_ssem.at[s], x_rsem.at[s],
+                      at(y, z, peer, k))
+
+    def x_all(s):
+        return all_of(x_recv.at[s], x_ssem.at[s], x_rsem.at[s])
 
     def b_copy(s, zz):
-        return remote(gath.at[s, xy], gath.at[s, xy], b_ssem.at[s, zz - 1], b_rsem.at[s],
+        return remote(gath.at[s, xy], gath.at[s, xy], b_ssem.at[s], b_rsem.at[s],
                       at(y, zh * NZL + zz, x, k))
 
     def g_copy(s, o):
         py, px = (y + o // NX) % NY, (x + o % NX) % NX
-        return remote(gath.at[s, xy], gath.at[s, xy], g_ssem.at[s, o - 1], g_rsem.at[s, o - 1],
+        return remote(gath.at[s, xy], gath.at[s, xy], g_ssem.at[s], g_rsem.at[s],
                       at(py, z, px, k))
 
-    def g_arrival(s, o):
-        py, px = (y + NY - o // NX) % NY, (x + NX - o % NX) % NX
-        there = py * NX + px
-        return remote(gath.at[s, there], gath.at[s, there], g_ssem.at[s, o - 1], g_rsem.at[s, o - 1],
-                      at(py, z, px, k))
+    def g_all(s):
+        return all_of(gath.at[s, pl.ds(0, NXY - 1)], g_ssem.at[s], g_rsem.at[s])
 
     def hub_step(s):
         total = exc_t[s, y] - z_send[s].astype(F32)
+        all_of(z_recv.at[s, pl.ds(0, NZ - 1)], z_ssem.at[s, 0], z_rsem.at[s]).wait_recv()
         for o in range(1, NZ):
-            far = (z + o) % NZ
-            remote(z_recv.at[s, far], z_recv.at[s, far], z_ssem.at[s, 0], z_rsem.at[s, far],
-                   partner).wait_recv()
-            total = total - z_recv[s, far].astype(F32)
+            total = total - z_recv[s, (z + o) % NZ].astype(F32)
         if s == 1:
-            for hh in range(2):
-                @pl.when(jnp.logical_not(cell0 & (zh == hh)))
-                def _():
-                    remote(d0_recv.at[hh], d0_recv.at[hh], d0_ssem.at[0], d0_rsem.at[hh],
-                           partner).wait_recv()
+            @pl.when(cell0)
+            def _():
+                all_of(d0_recv.at[1 - zh], d0_ssem, d0_rsem).wait_recv()
+
+            @pl.when(jnp.logical_not(cell0))
+            def _():
+                all_of(d0_recv, d0_ssem, d0_rsem).wait_recv()
+
             total = total - d0_recv[0].astype(F32) - d0_recv[1].astype(F32)
         rhs[s, k] = total.astype(BF16)
         rhs_copy(s).start()
@@ -241,14 +271,14 @@
         if s == 0:
             @pl.when(jnp.logical_not(cell0))
             def _():
-                h_pass(0)
+                partial_of_next()
         total = c_own[x]
+        x_all(s).wait_recv()
         for o in range(1, NX):
-            x_copy(s, o).wait_recv()
             total = total + x_recv[s, o - 1].astype(F32)
         gath[s, xy] = total.astype(BF16)
         if s == 1:
-            for zz in range(NZL - 1, 0, -1):
+            for zz in range(1, NZL):
                 b_copy(s, zz).start()
         for j in range(NY):
             oy = (NY - y + j) % NY
@@ -257,7 +287,7 @@
                 def _():
                     g_copy(s, oy * NX + ox).start()
         if s == 0:
-            for zz in range(NZL - 1, 0, -1):
+            for zz in range(1, NZL):
                 b_copy(s, zz).start()
 
     def relay(s):
@@ -266,16 +296,30 @@
             g_copy(s, o).start()
 
     def gathered(s):
-        for o in range(1, NXY):
-            g_arrival(s, o).wait_recv()
+        g_all(s).wait_recv()
 
     def whole(s):
         return gath[s].astype(F32).reshape(EXC, ROWS)
 
     def d0_copy(o, hh):
         peer = (y + o) % NY
-        return remote(d0_send.at[peer], d0_recv.at[zh], d0_ssem.at[o * 2 + hh], d0_rsem.at[zh],
+        return remote(d0_send.at[peer], d0_recv.at[zh], d0_ssem, d0_rsem,
                       at(peer, hh * NZL, x, k))
+
+    def partial_of_next():
+        h_whole(0)
+        past = older[0].astype(F32).T.astype(BF16)
+        mine = partial_sums(1, past)
+        core_copy(1).start()
+        own_half[1] = nt(past, dop[mine, :])
+
+    @pl.when(jnp.logical_not(cell0))
+    def _():
+        h_pass(0)
+
+        @pl.when(jnp.logical_not(hub))
+        def _():
+            partial_of_next()
 
     @pl.when(hub)
     def _():
@@ -298,15 +342,6 @@
 
     @pl.when(jnp.logical_not(cell0))
     def _():
-        @pl.when(jnp.logical_not(hub))
-        def _():
-            h_pass(0)
-
-        h_whole(0)
-        past = older[0].astype(F32).T.astype(BF16)
-        mine = partial_sums(1, past)
-        core_copy(1).start()
-        own_half[1] = nt(past, dop[mine, :])
         y_stage(1)
 
     z_stage(1)
@@ -360,8 +395,7 @@
 
         @pl.when(d > i)
         def _():
-            for o in range(1, NX):
-                hx_copy(i, o).wait_send()
+            hx_all(i).wait_send()
 
     core_copy(0).wait_send()
 
@@ -370,31 +404,24 @@
         core_copy(1).wait_send()
 
     for s in range(STEPS):
-        for o in range(1, NY):
-            y_copy(s, o).wait_send()
+        y_all(s).wait_send()
         for hh in range(2):
             @pl.when(z != hh * NZL)
             def _():
                 z_copy(s, hh).wait_send()
-        for o in range(1, NXY):
-            g_copy(s, o).wait_send()
+        g_all(s).wait_send()
 
     @pl.when(hub)
     def _():
         for s in range(STEPS):
             rhs_copy(s).wait_send()
-            for o in range(1, NX):
-                x_copy(s, o).wait_send()
-            for zz in range(1, NZL):
-                b_copy(s, zz).wait_send()
+            x_all(s).wait_send()
+            all_of(gath.at[s, pl.ds(0, NZL - 1)], b_ssem.at[s], b_rsem.at[s]).wait_send()
 
     @pl.when(cell0)
     def _():
         core_copy(2).wait_send()
-        for o in range(NY):
-            d0_copy(o, 1 - zh).wait_send()
-        for o in range(1, NY):
-            d0_copy(o, zh).wait_send()
+        all_of(z_recv.at[0, pl.ds(0, 2 * NY - 1)], d0_ssem, d0_rsem).wait_send()
 
 
 def store(cur, fin, cur_out, fin_out, sem):
@@ -437,24 +464,25 @@
             vmem((STEPS, NX - 1, XE, ROWS), BF16),
             vmem((STEPS, NXY, XE, ROWS), BF16),
             dma((3,)),
-            dma((6,)),
+            dma((2,)),
             dma((2, 2)),
-            dma((2, NX - 1)),
-            dma((2, NX - 1)),
+            dma((2,)),
+            dma((2,)),
             dma((3, 2)),
-            dma((STEPS, NY - 1)),
-            dma((STEPS, NY - 1)),
+            dma((STEPS,)),
+            dma((STEPS,)),
             dma((STEPS, 2)),
-            dma((STEPS, NZ)),
-            dma((8,)),
-            dma((2,)),
+            dma((STEPS,)),
+            dma,
+            dma,
             dma((STEPS, 2)),
-            dma((STEPS, NX - 1)),
-            dma((STEPS, NX - 1)),
-            dma((STEPS, NZL - 1)),
-            dma((STEPS,)),
-            dma((STEPS, NXY - 1)),
-            dma((STEPS, NXY - 1)),
+            dma((STEPS,)),
+            dma((STEPS,)),
+            dma((STEPS,)),
+            dma((STEPS,)),
+            dma((STEPS,)),
+            dma((STEPS,)),
+            pltpu.SemaphoreType.REGULAR,
         ],
         compiler_params=pltpu.CompilerParams(collective_id=0, has_side_effects=True),
     )(excitation, delay_ops, inverse_op, history)

time: 64.3 us -> 60.7 us (0.944)
  Pallas kernels: 63.5 us -> 59.9 us
    pallas_call x1, Pallas kernels: 62.7 us -> 59 us  [on_device(): pl.pallas_call(kernel, out_shape=(vmem((STEPS, ROWS, EXC), BF16), vmem((1...]
where the time goes in v3:
time: 60.7 us; the launch traced here: 60.5 us
  Pallas kernels  59.9 us (99%)
  between operations  0.64 us (1%)
    pallas_call x1, Pallas kernels, on_device(): pl.pallas_call(kernel, out_shape=(vmem((STEPS, ROWS, EXC), BF16), vmem((1...  59 us

profile of v3, /device:TPU:32, one launch (start us, length us, event | category | flops | bytes accessed | tf_op | source)
XLA Modules:
  0.0 60.5 jit_solution(11605468047235011812)
XLA Ops:
  0.6 59.0 %shard_map.59 = (bf16[2,768,128]{2,1,0:T(8,128)(2,1)S(1)}, bf16[1,768,128]{2,1,0:T(8,128)(2,1)S(1)}) custom-call(bf16[2,768,128]{2,1,0:T(8,128)(2,1)} %exc_in.1, bf16[1,768,768]{2,1,0:T(8,128)(2,1)} %d_in.1, bf16[768,768]{1,0:T(8,128)(2,1)} %inv_in.1, bf16[1,768,128]{2,1,0:T(8,128)(2,1)} %h_in.1), custom_call_target="tpu_custom_call" | custom-call | tf_op jit(solution)/shard_map/pallas_call | solution.py:440
  59.7 0.8 %shard_map.60 = (bf16[2,768,128]{2,1,0:T(8,128)(2,1)}, bf16[1,768,128]{2,1,0:T(8,128)(2,1)}) custom-call(bf16[2,768,128]{2,1,0:T(8,128)(2,1)S(1)} %get-tuple-element.4.cur, bf16[1,768,128]{2,1,0:T(8,128)(2,1)S(1)} %get-tuple-element.5.fin), custom_call_target="tpu_custom_call" | custom-call | tf_op jit(solution)/shard_map/pallas_call | solution.py:489

commit v4 on v3

--- a/solution.py
+++ b/solution.py
@@ -24,11 +24,11 @@
 
 
 def kernel(exc_in, d_in, inv_in, h_in, cur_out, fin_out,
-           exc, dop, inv, hist, older,
+           exc, dop, inv, inv_part, hist, older,
            core_send, core_recv, own_half, y_send, y_recv, z_send, z_recv,
-           d0_send, d0_recv, exc_t, rhs, c_own, x_send, x_recv, gath,
-           load_sem, d_sem, h_sem, hx_ssem, hx_rsem, core_sem, y_ssem, y_rsem, z_ssem, z_rsem,
-           d0_ssem, d0_rsem, rhs_sem, x_ssem, x_rsem, b_ssem, b_rsem, g_ssem, g_rsem, far_sem):
+           d0_send, d0_recv, exc_t, c_own, x_send, x_recv, gath,
+           load_sem, d_sem, inv_sem, h_sem, hx_ssem, hx_rsem, core_sem, y_ssem, y_rsem, z_ssem, z_rsem,
+           d0_ssem, d0_rsem, x_ssem, x_rsem, b_ssem, b_rsem, g_ssem, g_rsem, far_sem):
     d = lax.axis_index("delay")
     x = lax.axis_index("row")
     c = lax.axis_index("col")
@@ -56,7 +56,8 @@
     loads = [
         pltpu.make_async_copy(h_in.at[0], hist, load_sem.at[0]),
         pltpu.make_async_copy(exc_in, exc, load_sem.at[1]),
-        pltpu.make_async_copy(inv_in, inv, load_sem.at[2]),
+        pltpu.make_async_copy(inv_in.at[:, pl.ds(0, HALF)], inv.at[0], load_sem.at[2]),
+        pltpu.make_async_copy(inv_in.at[:, pl.ds(HALF, HALF)], inv.at[1], load_sem.at[3]),
     ]
     loads[0].start()
     for i in range(6):
@@ -182,8 +183,8 @@
     loads[0].wait()
     past = hist[...].astype(F32).T.astype(BF16)
     d_half(0, other).wait()
-    loads[1].start()
-    loads[2].start()
+    for load in loads[1:]:
+        load.start()
     mine = partial_sums(0, past)
     pl.semaphore_wait(barrier, peers)
 
@@ -201,11 +202,14 @@
     d_half(1, k).wait()
     own_half[0] = nt(past, dop[mine, :])
     y_stage(0)
-    loads[1].wait()
-    loads[2].wait()
+    for load in loads[1:]:
+        load.wait()
+
+    inv_copy = remote(inv.at[other], inv_part, inv_sem.at[0], inv_sem.at[1], partner)
 
     @pl.when(hub)
     def _():
+        inv_copy.start()
         rows = pl.ds(pl.multiple_of(k * HALF, HALF), HALF)
         for s in range(STEPS):
             exc_t[s] = exc[s, rows, :].astype(F32).T.reshape(NY, YE, HALF)
@@ -218,16 +222,10 @@
         for o in range(1, NY):
             y_copy(1, o).start()
 
-    def rhs_copy(s):
-        return remote(rhs.at[s, k], rhs.at[s, k], rhs_sem.at[s, 0], rhs_sem.at[s, 1], partner)
-
-    def rhs_arrival(s):
-        return remote(rhs.at[s, other], rhs.at[s, other], rhs_sem.at[s, 0], rhs_sem.at[s, 1], partner)
-
-    def x_copy(s, o):
+    def x_copy(s, o, kk):
         peer = (x + o) % NX
-        return remote(x_send.at[s, peer], x_recv.at[s, o - 1], x_ssem.at[s], x_rsem.at[s],
-                      at(y, z, peer, k))
+        return remote(x_send.at[s, kk, peer], x_recv.at[s, kk * NX + o - 1], x_ssem.at[s],
+                      x_rsem.at[s], at(y, z, peer, k if kk == 0 else other))
 
     def x_all(s):
         return all_of(x_recv.at[s], x_ssem.at[s], x_rsem.at[s])
@@ -259,30 +257,31 @@
                 all_of(d0_recv, d0_ssem, d0_rsem).wait_recv()
 
             total = total - d0_recv[0].astype(F32) - d0_recv[1].astype(F32)
-        rhs[s, k] = total.astype(BF16)
-        rhs_copy(s).start()
-        rhs_arrival(s).wait_recv()
-        product = nt(rhs[s, 0], inv[:, :HALF]) + nt(rhs[s, 1], inv[:, HALF:])
-        product = product.reshape(NX, XE, ROWS)
+        rhs = total.astype(BF16)
+        x_send[s, 1] = nt(rhs, inv_part[...]).reshape(NX, XE, ROWS).astype(BF16)
+        for o in (2, 1, 3, 0):
+            x_copy(s, o, 1).start()
+        product = nt(rhs, inv[k]).reshape(NX, XE, ROWS)
         c_own[...] = product
-        x_send[s] = product.astype(BF16)
-        for o in range(1, NX):
-            x_copy(s, o).start()
+        x_send[s, 0] = product.astype(BF16)
+        for o in (2, 1, 3):
+            x_copy(s, o, 0).start()
         if s == 0:
             @pl.when(jnp.logical_not(cell0))
             def _():
                 partial_of_next()
+                y_stage(1)
         total = c_own[x]
         x_all(s).wait_recv()
-        for o in range(1, NX):
-            total = total + x_recv[s, o - 1].astype(F32)
+        for i in range(2 * NX - 1):
+            total = total + x_recv[s, i].astype(F32)
         gath[s, xy] = total.astype(BF16)
         if s == 1:
             for zz in range(1, NZL):
                 b_copy(s, zz).start()
         for j in range(NY):
             oy = (NY - y + j) % NY
-            for ox in range(NX):
+            for ox in (2, 1, 3, 0):
                 @pl.when((oy != 0) | (ox != 0))
                 def _():
                     g_copy(s, oy * NX + ox).start()
@@ -292,7 +291,7 @@
 
     def relay(s):
         b_copy(s, 1).wait_recv()
-        for o in range(1, NXY):
+        for o in sorted(range(1, NXY), key=lambda o: -min(o % NX, -o % NX) - min(o // NX, -(o // NX) % NY)):
             g_copy(s, o).start()
 
     def gathered(s):
@@ -320,10 +319,14 @@
         @pl.when(jnp.logical_not(hub))
         def _():
             partial_of_next()
+            y_stage(1)
 
     @pl.when(hub)
     def _():
+        inv_copy.wait_recv()
         hub_step(0)
+
+    z_stage(1)
 
     @pl.when(cell0)
     def _():
@@ -340,12 +343,6 @@
         for o in range(1, NY):
             d0_copy(o, zh).start()
 
-    @pl.when(jnp.logical_not(cell0))
-    def _():
-        y_stage(1)
-
-    z_stage(1)
-
     @pl.when(d < 30)
     def _():
         h_copy(1).start()
@@ -413,8 +410,8 @@
 
     @pl.when(hub)
     def _():
+        inv_copy.wait_send()
         for s in range(STEPS):
-            rhs_copy(s).wait_send()
             x_all(s).wait_send()
             all_of(gath.at[s, pl.ds(0, NZL - 1)], b_ssem.at[s], b_rsem.at[s]).wait_send()
 
@@ -445,7 +442,8 @@
         scratch_shapes=[
             vmem((STEPS, ROWS, EXC), BF16),
             vmem((ROWS, ROWS), BF16),
-            vmem((ROWS, ROWS), BF16),
+            vmem((2, ROWS, HALF), BF16),
+            vmem((ROWS, HALF), BF16),
             vmem((ROWS, EXC), BF16),
             vmem((2, ROWS, EXC), BF16),
             vmem((3, EXC, HALF), BF16),
@@ -458,12 +456,12 @@
             vmem((NY, YE, HALF), BF16),
             vmem((2, YE, HALF), BF16),
             vmem((STEPS, NY, YE, HALF), F32),
-            vmem((STEPS, 2, YE, HALF), BF16),
             vmem((NX, XE, ROWS), F32),
-            vmem((STEPS, NX, XE, ROWS), BF16),
-            vmem((STEPS, NX - 1, XE, ROWS), BF16),
+            vmem((STEPS, 2, NX, XE, ROWS), BF16),
+            vmem((STEPS, 2 * NX - 1, XE, ROWS), BF16),
             vmem((STEPS, NXY, XE, ROWS), BF16),
-            dma((3,)),
+            dma((4,)),
+            dma((2,)),
             dma((2,)),
             dma((2, 2)),
             dma((2,)),
@@ -475,7 +473,6 @@
             dma((STEPS,)),
             dma,
             dma,
-            dma((STEPS, 2)),
             dma((STEPS,)),
             dma((STEPS,)),
             dma((STEPS,)),

time: 60.7 us -> 58.6 us (0.965)
  Pallas kernels: 59.9 us -> 57.8 us
    pallas_call x1, Pallas kernels: 59 us -> 57 us  [on_device(): pl.pallas_call(kernel, out_shape=(vmem((STEPS, ROWS, EXC), BF16), vmem((1...]
where the time goes in v4:
time: 58.6 us; the launch traced here: 58.5 us
  Pallas kernels  57.8 us (99%)
  between operations  0.64 us (1%)
    pallas_call x1, Pallas kernels, on_device(): pl.pallas_call(kernel, out_shape=(vmem((STEPS, ROWS, EXC), BF16), vmem((1...  57 us

profile of v4, /device:TPU:32, one launch (start us, length us, event | category | flops | bytes accessed | tf_op | source)
XLA Modules:
  0.0 58.5 jit_solution(17085364277193533640)
XLA Ops:
  0.6 57.0 %shard_map.59 = (bf16[2,768,128]{2,1,0:T(8,128)(2,1)S(1)}, bf16[1,768,128]{2,1,0:T(8,128)(2,1)S(1)}) custom-call(bf16[2,768,128]{2,1,0:T(8,128)(2,1)} %exc_in.1, bf16[1,768,768]{2,1,0:T(8,128)(2,1)} %d_in.1, bf16[768,768]{1,0:T(8,128)(2,1)} %inv_in.1, bf16[1,768,128]{2,1,0:T(8,128)(2,1)} %h_in.1), custom_call_target="tpu_custom_call" | custom-call | tf_op jit(solution)/shard_map/pallas_call | solution.py:437
  57.6 0.8 %shard_map.60 = (bf16[2,768,128]{2,1,0:T(8,128)(2,1)}, bf16[1,768,128]{2,1,0:T(8,128)(2,1)}) custom-call(bf16[2,768,128]{2,1,0:T(8,128)(2,1)S(1)} %get-tuple-element.4.cur, bf16[1,768,128]{2,1,0:T(8,128)(2,1)S(1)} %get-tuple-element.5.fin), custom_call_target="tpu_custom_call" | custom-call | tf_op jit(solution)/shard_map/pallas_call | solution.py:486
